TPU v7x, 32 devices: a whole 2x2x4 slice. The times are simulated.
32 devices in a mesh: dp: 4 (over x, core), space: 8 (over z, y).
Axes of the slice: x: 2, y: 2, z: 4, core: 2. Of those that a mesh axis runs over, the one named last changes fastest.
Arguments:
- section_three: bfloat16 [4, 64, 128, 512], P('dp', 'space'), parts along dimension 0, may hold values from -6 to 6
- section_four: bfloat16 [4, 32, 64, 1024], P('dp', 'space'), parts along dimension 0, may hold values from -6 to 6
- section_five: bfloat16 [4, 16, 32, 2048], P('dp', 'space'), parts along dimension 0, may hold values from -6 to 6
- lateral_three: bfloat16 [512, 256], P('space'), may hold values from -0.25 to 0.25
- lateral_four: bfloat16 [1024, 256], P('space'), may hold values from -0.1875 to 0.1875
- lateral_five: bfloat16 [2048, 256], P('space'), may hold values from -0.125 to 0.125
- lateral_bias_three: float32 [256], replicated, may hold values from -3 to 3
- lateral_bias_four: float32 [256], replicated, may hold values from -3 to 3
- lateral_bias_five: float32 [256], replicated, may hold values from -3 to 3
- output_three: bfloat16 [3, 3, 256, 256], P(None, None, 'space'), may hold values from -0.125 to 0.125
- output_four: bfloat16 [3, 3, 256, 256], P(None, None, 'space'), may hold values from -0.125 to 0.125
- output_five: bfloat16 [3, 3, 256, 256], P(None, None, 'space'), may hold values from -0.125 to 0.125
- output_bias_three: float32 [256], replicated, may hold values from -3 to 3
- output_bias_four: float32 [256], replicated, may hold values from -3 to 3
- output_bias_five: float32 [256], replicated, may hold values from -3 to 3
Outputs:
- level_three: bfloat16 [4, 64, 128, 256], P('dp', 'space'), parts along dimension 0
- level_four: bfloat16 [4, 32, 64, 256], P('dp', 'space'), parts along dimension 0
- level_five: bfloat16 [4, 16, 32, 256], P('dp'), parts along dimension 0
- level_six: bfloat16 [4, 8, 16, 256], P('dp'), parts along dimension 0
There are 4 independent parts, one for each index of `dp`. A program takes and returns all parts, laid end to end along the dimension named above; an argument that names none is the same for every part. Nothing has to cross between parts.
All inputs are finite; a program needn't handle non-finite values.
Results may differ from a plain program's by a relative error of at most 0.0095.
Values may be sent and summed in bfloat16 or wider, within the bound.
A program may use at most 64 MiB of HBM per device.

v0:
```python
import jax
import jax.numpy as jnp
from jax import lax
from jax.sharding import PartitionSpec as P


def with_halo(cells, sides, width):
    for axis, dim in sides:
        count = lax.axis_size(axis)
        ends = count - 1
        head = lax.slice_in_dim(cells, 0, width, axis=dim)
        tail = lax.slice_in_dim(cells, cells.shape[dim] - width, cells.shape[dim], axis=dim)
        cells = jnp.concatenate(
            [
                lax.ppermute(tail, axis, [(i, (i + 1) % count) for i in range(ends)]),
                cells,
                lax.ppermute(head, axis, [((i + 1) % count, i) for i in range(ends)]),
            ],
            axis=dim,
        )
    return cells


def lateral(features, weight, offset):
    images, rows, columns, channels = features.shape
    summed = (
        jnp.dot(features.reshape(-1, channels), weight, preferred_element_type=jnp.float32) + offset
    )
    return summed.reshape(images, rows, columns, -1)


def enlarge(coarse):
    return jnp.repeat(jnp.repeat(coarse, 2, axis=1), 2, axis=2)


def conv_rows(padded, weight, offset):
    images, rows_in, columns, channels = padded.shape
    height = rows_in - 2
    framed = jnp.pad(padded, ((0, 0), (0, 0), (1, 1), (0, 0)))
    summed = jnp.zeros((images * height * columns, weight.shape[3]), jnp.float32)
    for row_off in range(3):
        for col_off in range(3):
            window = framed[:, row_off : row_off + height, col_off : col_off + columns, :].reshape(
                -1, channels
            )
            summed = summed + jnp.dot(
                window, weight[row_off, col_off], preferred_element_type=jnp.float32
            )
    return (summed + offset).reshape(images, height, columns, -1).astype(jnp.bfloat16)


def on_device(
    section_three,
    section_four,
    section_five,
    lateral_three,
    lateral_four,
    lateral_five,
    lateral_bias_three,
    lateral_bias_four,
    lateral_bias_five,
    output_three,
    output_four,
    output_five,
    output_bias_three,
    output_bias_four,
    output_bias_five,
):
    whole_lat3, whole_lat4, whole_lat5, whole_out3, whole_out4, whole_out5 = (
        lax.all_gather(lateral_three, "space", axis=0, tiled=True),
        lax.all_gather(lateral_four, "space", axis=0, tiled=True),
        lax.all_gather(lateral_five, "space", axis=0, tiled=True),
        lax.all_gather(output_three, "space", axis=2, tiled=True),
        lax.all_gather(output_four, "space", axis=2, tiled=True),
        lax.all_gather(output_five, "space", axis=2, tiled=True),
    )
    merged_five = lateral(section_five, whole_lat5, lateral_bias_five).astype(jnp.bfloat16)
    merged_four = (
        lateral(section_four, whole_lat4, lateral_bias_four)
        + enlarge(merged_five).astype(jnp.float32)
    ).astype(jnp.bfloat16)
    merged_three = (
        lateral(section_three, whole_lat3, lateral_bias_three)
        + enlarge(merged_four).astype(jnp.float32)
    ).astype(jnp.bfloat16)
    rimmed_three = with_halo(merged_three, (("space", 1),), 1)
    rimmed_four = with_halo(merged_four, (("space", 1),), 1)
    level_three = conv_rows(rimmed_three, whole_out3, output_bias_three)
    level_four = conv_rows(rimmed_four, whole_out4, output_bias_four)
    whole_five = lax.all_gather(merged_five, "space", axis=1, tiled=True)
    padded_five = jnp.pad(whole_five, ((0, 0), (1, 1), (0, 0), (0, 0)))
    level_five = conv_rows(padded_five, whole_out5, output_bias_five)
    level_six = level_five[:, ::2, ::2, :]
    return (level_three, level_four, level_five, level_six)


def solution(mesh):
    return jax.shard_map(
        on_device,
        mesh=mesh,
        in_specs=(
            P("dp", "space", None, None),
            P("dp", "space", None, None),
            P("dp", "space", None, None),
            P("space", None),
            P("space", None),
            P("space", None),
            P(),
            P(),
            P(),
            P(None, None, "space", None),
            P(None, None, "space", None),
            P(None, None, "space", None),
            P(),
            P(),
            P(),
        ),
        out_specs=(
            P("dp", "space", None, None),
            P("dp", "space", None, None),
            P("dp", None, None, None),
            P("dp", None, None, None),
        ),
        check_vma=False,
    )
```

profile of v0, /device:TPU:0, one launch (start us, length us, event | category | flops | bytes accessed | tf_op | source)
XLA Modules:
  0.0 203.1 jit_solution(6566703507592191311)
XLA Ops:
  10.0 33.9 %all_gather.22 = bf16[1024,256]{1,0:T(8,128)(2,1)S(1)} all-gather(bf16[128,256]{1,0:T(8,128)(2,1)} %param.19), channel_id=1, replica_groups=mesh['dp'=4,'space'=8] {'space'}, dimensions={0}, use_global_device_ids=true | all-gather | bytes 589824 | tf_op jit(solution)/shard_map/all_gather | solution.py:71
  43.9 30.8 %all_gather.21 = bf16[512,256]{1,0:T(8,128)(2,1)S(1)} all-gather(bf16[64,256]{1,0:T(8,128)(2,1)S(1)} %copy-done.36), channel_id=1, replica_groups=mesh['dp'=4,'space'=8] {'space'}, dimensions={0}, use_global_device_ids=true | all-gather | bytes 294912 | tf_op jit(solution)/shard_map/all_gather | solution.py:70
  76.0 1.5 fusion.9
  79.4 4.7 %collective-permute-start.2 = (bf16[1,1,64,256]{3,2,1,0:T(8,128)(2,1)}, bf16[1,1,64,256]{3,2,1,0:T(8,128)(2,1)}, u32[]{:S(2)}, u32[]{:S(2)}) collective-permute-start(bf16[1,1,64,256]{3,2,1,0:T(8,128)(2,1)} %get-tuple-element.30), channel_id=1, source_target_pairs={{0,1},{1,2},{2,3},{3,4},{4,5},{5,6},{6,7},{8,9},{9,10},{10,11},{11... | collective-permute-start | bytes 98312 | tf_op jit(solution)/shard_map/ppermute | solution.py:15
  84.1 1.3 collective-permute-start.3
  85.8 1.7 convert_element_type.169
  87.6 1.3 add_convert_fusion.1
  90.4 5.2 %collective-permute-start = (bf16[1,1,128,256]{3,2,1,0:T(8,128)(2,1)}, bf16[1,1,128,256]{3,2,1,0:T(8,128)(2,1)}, u32[]{:S(2)}, u32[]{:S(2)}) collective-permute-start(bf16[1,1,128,256]{3,2,1,0:T(8,128)(2,1)} %get-tuple-element.12), channel_id=1, source_target_pairs={{0,1},{1,2},{2,3},{3,4},{4,5},{5,6},{6,7},{8,9},{9,10},{10,11},{11... | collective-permute-start | bytes 196616 | tf_op jit(solution)/shard_map/ppermute | solution.py:15
  95.6 1.3 collective-permute-start.1
  96.8 31.6 %all_gather.26 = bf16[1,16,32,256]{3,2,0,1:T(8,128)(2,1)S(1)} all-gather(bf16[1,2,32,256]{3,2,0,1:T(8,128)(2,1)S(1)} %bitcast.189), channel_id=1, replica_groups=mesh['dp'=4,'space'=8] {'space'}, dimensions={1}, use_global_device_ids=true | all-gather | bytes 294912 | tf_op jit(solution)/shard_map/all_gather | solution.py:90
  128.5 1.3 pad_slice_fusion
  130.7 1.9 convert_element_type.177
  132.6 1.7 convert_element_type.171
  136.1 1.5 pad_maximum_fusion.2
  138.7 1.6 fusion.27
  140.3 1.9 pad_maximum_fusion
  142.2 1.3 fusion.22
  143.6 1.2 convolution_add_fusion.15
  147.5 2.5 %slice.239 = bf16[1,8,16,256]{3,2,1,0:T(8,128)(2,1)} slice(bf16[1,16,32,256]{3,2,1,0:T(8,128)(2,1)S(1)} %bitcast.186), slice={[0:1:1], [0:16:2], [0:32:2], [0:256:1]} | slice | bytes 131072 | tf_op jit(solution)/shard_map/slice | solution.py:93
  150.1 1.1 fusion.24
  151.2 1.8 fusion.23
  153.1 30.5 %all-gather.7.cloned.1.call-done = bf16[3,3,256,256]{3,2,1,0:T(8,128)(2,1)} async-done(((bf16[3,3,32,256]{3,2,1,0:T(8,128)(2,1)}), bf16[3,3,256,256]{3,2,1,0:T(8,128)(2,1)}) %all-gather.7.cloned.1.call-update) | async-done | bytes 1179664 | tf_op jit(solution)/shard_map/all_gather | solution.py:73
  183.5 1.3 fusion.26
  195.5 1.1 fusion.3
  (139 shorter events, 24.6 us)
Async XLA Ops:
  7.2 67.8 %copy-start = (bf16[1,8,128,512]{3,2,1,0:T(8,128)(2,1)S(1)}, bf16[1,8,128,512]{3,2,1,0:T(8,128)(2,1)}, u32[]{:S(2)}) copy-start(bf16[1,8,128,512]{3,2,1,0:T(8,128)(2,1)} %param.15) | copy-start | bytes 3145732
  7.2 36.7 %copy-start.36 = (bf16[64,256]{1,0:T(8,128)(2,1)S(1)}, bf16[64,256]{1,0:T(8,128)(2,1)}, u32[]{:S(2)}) copy-start(bf16[64,256]{1,0:T(8,128)(2,1)} %param.18) | copy-start | bytes 98308
  7.2 67.5 %copy-start.24 = (bf16[1,4,64,1024]{3,2,1,0:T(8,128)(2,1)S(1)}, bf16[1,4,64,1024]{3,2,1,0:T(8,128)(2,1)}, u32[]{:S(2)}) copy-start(bf16[1,4,64,1024]{3,2,1,0:T(8,128)(2,1)} %param.16) | copy-start | bytes 1572868
  7.2 67.5 %copy-start.40 = (f32[256]{0:T(256)S(1)}, f32[256]{0:T(256)}, u32[]{:S(2)}) copy-start(f32[256]{0:T(256)} %param.22) | copy-start | bytes 3076
  7.2 68.3 %all-gather.5.cloned.1.call-start = ((), (), s32[]{:S(2)}) async-start(), calls=%async_computation | async-start | bytes 1179648 | tf_op jit(solution)/shard_map/all_gather | solution.py:72
  7.9 134.3 %all-gather.11.cloned.1.call-start = ((), (), s32[]{:S(2)}) async-start(), calls=%async_computation.3 | async-start | bytes 1327104 | tf_op jit(solution)/shard_map/all_gather | solution.py:75
  8.7 141.4 %all-gather.9.cloned.1.call-start = ((), (), s32[]{:S(2)}) async-start(), calls=%async_computation.2 | async-start | bytes 1327104 | tf_op jit(solution)/shard_map/all_gather | solution.py:74
  9.4 65.6 %copy-start.37 = (f32[256]{0:T(256)S(1)}, f32[256]{0:T(256)}, u32[]{:S(2)}) copy-start(f32[256]{0:T(256)} %param.21) | copy-start | bytes 3076
  9.4 174.1 %all-gather.7.cloned.1.call-start = ((), (), s32[]{:S(2)}) async-start(), calls=%async_computation.1 | async-start | bytes 1327104 | tf_op jit(solution)/shard_map/all_gather | solution.py:73
  75.0 10.4 %copy-start.4 = (f32[256,256]{1,0:T(8,128)}, f32[256,256]{1,0:T(8,128)S(1)}, u32[]{:S(2)}) copy-start(f32[256,256]{1,0:T(8,128)S(1)} %convolution_add_fusion.23) | copy-start | bytes 786436
  78.3 7.1 %copy-start.3 = (f32[4,32,2,256]{3,2,1,0:T(2,128)}, f32[4,32,2,256]{3,2,1,0:T(2,128)S(1)}, u32[]{:S(2)}) copy-start(f32[4,32,2,256]{3,2,1,0:T(2,128)S(1)} %broadcast_in_dim.9) | copy-start | bytes 786436
  79.4 55.0 %collective-permute-start.2 = (bf16[1,1,64,256]{3,2,1,0:T(8,128)(2,1)}, bf16[1,1,64,256]{3,2,1,0:T(8,128)(2,1)}, u32[]{:S(2)}, u32[]{:S(2)}) collective-permute-start(bf16[1,1,64,256]{3,2,1,0:T(8,128)(2,1)} %get-tuple-element.30), channel_id=1, source_target_pairs={{0,1},{1,2},{2,3},{3,4},{4,5},{5,6},{6,7},{8,9},{9,10},{10,11},{11... | collective-permute-start | bytes 98312 | tf_op jit(solution)/shard_map/ppermute | solution.py:15
  84.1 50.2 %collective-permute-start.3 = (bf16[1,1,64,256]{3,2,1,0:T(8,128)(2,1)}, bf16[1,1,64,256]{3,2,1,0:T(8,128)(2,1)}, u32[]{:S(2)}, u32[]{:S(2)}) collective-permute-start(bf16[1,1,64,256]{3,2,1,0:T(8,128)(2,1)} %get-tuple-element.31), channel_id=1, source_target_pairs={{1,0},{2,1},{3,2},{4,3},{5,4},{6,5},{7,6},{9,8},{10,9},{11,10},{12... | collective-permute-start | bytes 98312 | tf_op jit(solution)/shard_map/ppermute | solution.py:17
  87.6 9.3 %copy-start.34 = (bf16[64,256]{1,0:T(8,128)(2,1)S(1)}, bf16[64,256]{1,0:T(8,128)(2,1)}, u32[]{:S(2)}) copy-start(bf16[64,256]{1,0:T(8,128)(2,1)} %copy-done.33) | copy-start | bytes 98308
  90.4 47.2 %collective-permute-start = (bf16[1,1,128,256]{3,2,1,0:T(8,128)(2,1)}, bf16[1,1,128,256]{3,2,1,0:T(8,128)(2,1)}, u32[]{:S(2)}, u32[]{:S(2)}) collective-permute-start(bf16[1,1,128,256]{3,2,1,0:T(8,128)(2,1)} %get-tuple-element.12), channel_id=1, source_target_pairs={{0,1},{1,2},{2,3},{3,4},{4,5},{5,6},{6,7},{8,9},{9,10},{10,11},{11... | collective-permute-start | bytes 196616 | tf_op jit(solution)/shard_map/ppermute | solution.py:15
  95.6 42.1 %collective-permute-start.1 = (bf16[1,1,128,256]{3,2,1,0:T(8,128)(2,1)}, bf16[1,1,128,256]{3,2,1,0:T(8,128)(2,1)}, u32[]{:S(2)}, u32[]{:S(2)}) collective-permute-start(bf16[1,1,128,256]{3,2,1,0:T(8,128)(2,1)} %get-tuple-element.13), channel_id=1, source_target_pairs={{1,0},{2,1},{3,2},{4,3},{5,4},{6,5},{7,6},{9,8},{10,9},{11,10},{12... | collective-permute-start | bytes 196616 | tf_op jit(solution)/shard_map/ppermute | solution.py:17
  134.3 3.3 %copy-start.2 = (bf16[1,8,128,256]{3,2,1,0:T(8,128)(2,1)S(1)}, bf16[1,8,128,256]{3,2,1,0:T(8,128)(2,1)}, u32[]{:S(2)}) copy-start(bf16[1,8,128,256]{3,2,1,0:T(8,128)(2,1)} %copy-done.1) | copy-start | bytes 1572868
  142.2 2.6 %copy-start.14 = (bf16[3,3,256,256]{3,2,1,0:T(8,128)(2,1)S(1)}, bf16[3,3,256,256]{3,2,1,0:T(8,128)(2,1)}, u32[]{:S(2)}) copy-start(bf16[3,3,256,256]{3,2,1,0:T(8,128)(2,1)} %all-gather.11.cloned.1.call-done) | copy-start | bytes 3538948
  142.2 2.6 %copy-start.21 = (bf16[1,16,32,256]{3,2,0,1:T(8,128)(2,1)S(1)}, bf16[1,16,32,256]{3,2,0,1:T(8,128)(2,1)}, u32[]{:S(2)}) copy-start(bf16[1,16,32,256]{3,2,0,1:T(8,128)(2,1)} %get-tuple-element.17) | copy-start | bytes 786436
  143.6 1.5 copy-start.20
  147.2 4.0 %copy-start.31 = (bf16[1,4,64,256]{3,2,1,0:T(8,128)(2,1)S(1)}, bf16[1,4,64,256]{3,2,1,0:T(8,128)(2,1)}, u32[]{:S(2)}) copy-start(bf16[1,4,64,256]{3,2,1,0:T(8,128)(2,1)} %get-tuple-element.27) | copy-start | bytes 393220
  147.5 2.6 %copy-start.32 = (bf16[512,256]{1,0:T(8,128)(2,1)}, bf16[512,256]{1,0:T(8,128)(2,1)S(1)}, u32[]{:S(2)}) copy-start(bf16[512,256]{1,0:T(8,128)(2,1)S(1)} %fusion.5) | copy-start | bytes 786436
  193.6 1.8 copy-start.11
  193.7 1.8 copy-start.39
  (27 other events, 28.3 us)
Sparse Core Ops, SparseCore 0:
  10.1 44.0 all-gather.4
  56.4 42.5 all-gather.10
  101.2 40.1 all-gather.8
  143.5 39.9 all-gather.6
where the time goes:
time: 204 us; the launch traced here: 203 us
  blocking collectives  96.2 us (47%)
  waiting for transfers between devices  33.1 us (16%)
  local copies, waits for them, and re-layouts  24.3 us (12%)
  matrix products  15.8 us (8%)
  between operations  14.3 us (7%)
  starting transfers between devices  12.6 us (6%)
  other arithmetic  6.78 us (3%)
    all_gather x1, blocking collectives, on_device(): lax.all_gather(lateral_four, 'space', axis=0, tiled=True)  33.9 us
    all_gather x1, blocking collectives, on_device(): whole_five = lax.all_gather(merged_five, 'space', axis=1, tiled=True)  31.6 us
    all_gather x1, blocking collectives, on_device(): lax.all_gather(lateral_three, 'space', axis=0, tiled=True)  30.8 us
    all_gather x1, waiting for transfers between devices, on_device(): lax.all_gather(output_three, 'space', axis=2, tiled=True)  30.5 us
    dot_general x27, matrix products, conv_rows(): jnp.dot(window, weight[row_off, col_off], preferred_element_type=jnp.floa...  13.5 us
    ppermute x2, starting transfers between devices, with_halo(): lax.ppermute(tail, axis, [(i, (i + 1) % count) for i in range(ends)])  9.9 us
    unnamed x86, local copies, waits for them, and re-layouts  9.46 us
    concatenate x4, other arithmetic, with_halo(): jnp.concatenate([lax.ppermute(tail, axis, [(i, (i + 1) % count) for i in...  5.37 us
  transfers between devices with their start and end apart: 8, of which 1 were waited for; matrix products, arithmetic and copies ran while one was open for 15% of the time, Pallas kernels for 0%

commit v1 on v0

--- a/solution.py
+++ b/solution.py
@@ -70,7 +70,7 @@
         lax.all_gather(lateral_three, "space", axis=0, tiled=True),
         lax.all_gather(lateral_four, "space", axis=0, tiled=True),
         lax.all_gather(lateral_five, "space", axis=0, tiled=True),
-        lax.all_gather(output_three, "space", axis=2, tiled=True),
+        jnp.concatenate(lax.all_gather(output_three, "space"), axis=2),
         lax.all_gather(output_four, "space", axis=2, tiled=True),
         lax.all_gather(output_five, "space", axis=2, tiled=True),
     )

time: 204 us -> 197 us (0.966)
  waiting for transfers between devices: 33.1 us -> 26.1 us
    all_gather x1, waiting for transfers between devices: 30.5 us -> 0.01 us  [on_device(): lax.all_gather(output_three, 'space')]
    all_gather x1, waiting for transfers between devices: 0.01 us -> 21.7 us  [on_device(): lax.all_gather(output_four, 'space', axis=2, tiled=True)]
    unnamed x86 -> x84, local copies, waits for them, and re-layouts: 9.46 us -> 7.63 us
  transfers between devices with their start and end apart: 8 -> 8, of which waited for: 1 -> 2; matrix products, arithmetic and copies ran while one was open for 15% -> 17% of each run, Pallas kernels for 0% -> 0%
where the time goes in v1:
time: 197 us; the launch traced here: 196 us
  blocking collectives  95.5 us (48%)
  waiting for transfers between devices  26.1 us (13%)
  local copies, waits for them, and re-layouts  23.9 us (12%)
  matrix products  16.2 us (8%)
  between operations  14.4 us (7%)
  starting transfers between devices  12.7 us (6%)
  other arithmetic  6.64 us (3%)
    all_gather x1, blocking collectives, on_device(): lax.all_gather(lateral_four, 'space', axis=0, tiled=True)  33.9 us
    all_gather x1, blocking collectives, on_device(): whole_five = lax.all_gather(merged_five, 'space', axis=1, tiled=True)  30.9 us
    all_gather x1, blocking collectives, on_device(): lax.all_gather(lateral_three, 'space', axis=0, tiled=True)  30.8 us
    all_gather x1, waiting for transfers between devices, on_device(): lax.all_gather(output_four, 'space', axis=2, tiled=True)  21.7 us
    dot_general x27, matrix products, conv_rows(): jnp.dot(window, weight[row_off, col_off], preferred_element_type=jnp.floa...  14 us
    ppermute x2, starting transfers between devices, with_halo(): lax.ppermute(tail, axis, [(i, (i + 1) % count) for i in range(ends)])  9.87 us
    unnamed x84, local copies, waits for them, and re-layouts  7.63 us
    concatenate x4, other arithmetic, with_halo(): jnp.concatenate([lax.ppermute(tail, axis, [(i, (i + 1) % count) for i in...  5.23 us
  transfers between devices with their start and end apart: 8, of which 2 were waited for; matrix products, arithmetic and copies ran while one was open for 17% of the time, Pallas kernels for 0%

profile of v1, /device:TPU:0, one launch (start us, length us, event | category | flops | bytes accessed | tf_op | source)
XLA Modules:
  0.0 195.5 jit_solution(2938980113236783174)
XLA Ops:
  10.0 33.9 %all_gather.25 = bf16[1024,256]{1,0:T(8,128)(2,1)S(1)} all-gather(bf16[128,256]{1,0:T(8,128)(2,1)} %param.19), channel_id=1, replica_groups=mesh['dp'=4,'space'=8] {'space'}, dimensions={0}, use_global_device_ids=true | all-gather | bytes 589824 | tf_op jit(solution)/shard_map/all_gather | solution.py:71
  43.9 30.8 %all_gather.24 = bf16[512,256]{1,0:T(8,128)(2,1)S(1)} all-gather(bf16[64,256]{1,0:T(8,128)(2,1)S(1)} %copy-done.35), channel_id=1, replica_groups=mesh['dp'=4,'space'=8] {'space'}, dimensions={0}, use_global_device_ids=true | all-gather | bytes 294912 | tf_op jit(solution)/shard_map/all_gather | solution.py:70
  76.0 1.5 fusion.9
  78.7 4.7 %collective-permute-start.2 = (bf16[1,1,64,256]{3,2,1,0:T(8,128)(2,1)}, bf16[1,1,64,256]{3,2,1,0:T(8,128)(2,1)}, u32[]{:S(2)}, u32[]{:S(2)}) collective-permute-start(bf16[1,1,64,256]{3,2,1,0:T(8,128)(2,1)} %get-tuple-element.30), channel_id=1, source_target_pairs={{0,1},{1,2},{2,3},{3,4},{4,5},{5,6},{6,7},{8,9},{9,10},{10,11},{11... | collective-permute-start | bytes 98312 | tf_op jit(solution)/shard_map/ppermute | solution.py:15
  83.5 1.3 collective-permute-start.3
  85.2 1.7 convert_element_type.169
  86.9 1.3 add_convert_fusion.1
  89.7 5.2 %collective-permute-start = (bf16[1,1,128,256]{3,2,1,0:T(8,128)(2,1)}, bf16[1,1,128,256]{3,2,1,0:T(8,128)(2,1)}, u32[]{:S(2)}, u32[]{:S(2)}) collective-permute-start(bf16[1,1,128,256]{3,2,1,0:T(8,128)(2,1)} %get-tuple-element.12), channel_id=1, source_target_pairs={{0,1},{1,2},{2,3},{3,4},{4,5},{5,6},{6,7},{8,9},{9,10},{10,11},{11... | collective-permute-start | bytes 196616 | tf_op jit(solution)/shard_map/ppermute | solution.py:15
  94.9 30.9 %all_gather.30 = bf16[1,16,32,256]{3,2,0,1:T(8,128)(2,1)S(1)} all-gather(bf16[1,2,32,256]{3,2,0,1:T(8,128)(2,1)S(1)} %bitcast.203), channel_id=1, replica_groups=mesh['dp'=4,'space'=8] {'space'}, dimensions={1}, use_global_device_ids=true | all-gather | bytes 294912 | tf_op jit(solution)/shard_map/all_gather | solution.py:90
  125.8 1.3 pad_slice_fusion
  128.0 1.8 convert_element_type.177
  129.8 1.7 convert_element_type.171
  131.5 1.4 collective-permute-start.1
  134.7 1.5 pad_maximum_fusion.2
  136.2 1.8 collective-permute-done.1
  139.0 1.8 fusion.27
  140.9 1.9 pad_maximum_fusion
  142.7 1.4 copy.20
  144.2 1.3 fusion.22
  145.5 1.2 convolution_add_fusion.15
  149.4 2.5 %slice.239 = bf16[1,8,16,256]{3,2,1,0:T(8,128)(2,1)} slice(bf16[1,16,32,256]{3,2,1,0:T(8,128)(2,1)S(1)} %bitcast.200), slice={[0:1:1], [0:16:2], [0:32:2], [0:256:1]} | slice | bytes 131072 | tf_op jit(solution)/shard_map/slice | solution.py:93
  152.0 1.4 fusion.26
  161.3 21.7 %all-gather.8.cloned.1.call-done = bf16[3,3,256,256]{3,2,1,0:T(8,128)(2,1)} async-done(((bf16[3,3,32,256]{3,2,1,0:T(8,128)(2,1)}), bf16[3,3,256,256]{3,2,1,0:T(8,128)(2,1)}) %all-gather.8.cloned.1.call-update) | async-done | bytes 1179664 | tf_op jit(solution)/shard_map/all_gather | solution.py:74
  185.3 1.2 convolution_add_fusion.22
  (138 shorter events, 25.8 us)
Async XLA Ops:
  7.2 67.8 %copy-start = (bf16[1,8,128,512]{3,2,1,0:T(8,128)(2,1)S(1)}, bf16[1,8,128,512]{3,2,1,0:T(8,128)(2,1)}, u32[]{:S(2)}) copy-start(bf16[1,8,128,512]{3,2,1,0:T(8,128)(2,1)} %param.15) | copy-start | bytes 3145732
  7.2 36.7 %copy-start.35 = (bf16[64,256]{1,0:T(8,128)(2,1)S(1)}, bf16[64,256]{1,0:T(8,128)(2,1)}, u32[]{:S(2)}) copy-start(bf16[64,256]{1,0:T(8,128)(2,1)} %param.18) | copy-start | bytes 98308
  7.2 67.5 %copy-start.23 = (bf16[1,4,64,1024]{3,2,1,0:T(8,128)(2,1)S(1)}, bf16[1,4,64,1024]{3,2,1,0:T(8,128)(2,1)}, u32[]{:S(2)}) copy-start(bf16[1,4,64,1024]{3,2,1,0:T(8,128)(2,1)} %param.16) | copy-start | bytes 1572868
  7.2 67.4 %copy-start.39 = (f32[256]{0:T(256)S(1)}, f32[256]{0:T(256)}, u32[]{:S(2)}) copy-start(f32[256]{0:T(256)} %param.22) | copy-start | bytes 3076
  7.2 68.3 %all-gather.6.cloned.1.call-start = ((), (), s32[]{:S(2)}) async-start(), calls=%async_computation | async-start | bytes 1179648 | tf_op jit(solution)/shard_map/all_gather | solution.py:72
  7.9 134.8 %all-gather.12.cloned.1.call-start = ((), (), s32[]{:S(2)}) async-start(), calls=%async_computation.3 | async-start | bytes 1327104 | tf_op jit(solution)/shard_map/all_gather | solution.py:73
  8.7 135.4 %all-gather.10.cloned.1.call-start = ((), (), s32[]{:S(2)}) async-start(), calls=%async_computation.2 | async-start | bytes 1327104 | tf_op jit(solution)/shard_map/all_gather | solution.py:75
  9.4 65.6 %copy-start.36 = (f32[256]{0:T(256)S(1)}, f32[256]{0:T(256)}, u32[]{:S(2)}) copy-start(f32[256]{0:T(256)} %param.21) | copy-start | bytes 3076
  9.4 173.5 %all-gather.8.cloned.1.call-start = ((), (), s32[]{:S(2)}) async-start(), calls=%async_computation.1 | async-start | bytes 1327104 | tf_op jit(solution)/shard_map/all_gather | solution.py:74
  75.0 9.8 %copy-start.4 = (f32[256,256]{1,0:T(8,128)}, f32[256,256]{1,0:T(8,128)S(1)}, u32[]{:S(2)}) copy-start(f32[256,256]{1,0:T(8,128)S(1)} %convolution_add_fusion.23) | copy-start | bytes 786436
  77.7 7.1 %copy-start.3 = (f32[4,32,2,256]{3,2,1,0:T(2,128)}, f32[4,32,2,256]{3,2,1,0:T(2,128)S(1)}, u32[]{:S(2)}) copy-start(f32[4,32,2,256]{3,2,1,0:T(2,128)S(1)} %broadcast_in_dim.9) | copy-start | bytes 786436
  78.7 54.2 %collective-permute-start.2 = (bf16[1,1,64,256]{3,2,1,0:T(8,128)(2,1)}, bf16[1,1,64,256]{3,2,1,0:T(8,128)(2,1)}, u32[]{:S(2)}, u32[]{:S(2)}) collective-permute-start(bf16[1,1,64,256]{3,2,1,0:T(8,128)(2,1)} %get-tuple-element.30), channel_id=1, source_target_pairs={{0,1},{1,2},{2,3},{3,4},{4,5},{5,6},{6,7},{8,9},{9,10},{10,11},{11... | collective-permute-start | bytes 98312 | tf_op jit(solution)/shard_map/ppermute | solution.py:15
  83.5 49.5 %collective-permute-start.3 = (bf16[1,1,64,256]{3,2,1,0:T(8,128)(2,1)}, bf16[1,1,64,256]{3,2,1,0:T(8,128)(2,1)}, u32[]{:S(2)}, u32[]{:S(2)}) collective-permute-start(bf16[1,1,64,256]{3,2,1,0:T(8,128)(2,1)} %get-tuple-element.31), channel_id=1, source_target_pairs={{1,0},{2,1},{3,2},{4,3},{5,4},{6,5},{7,6},{9,8},{10,9},{11,10},{12... | collective-permute-start | bytes 98312 | tf_op jit(solution)/shard_map/ppermute | solution.py:17
  86.9 8.0 %copy-start.33 = (bf16[64,256]{1,0:T(8,128)(2,1)S(1)}, bf16[64,256]{1,0:T(8,128)(2,1)}, u32[]{:S(2)}) copy-start(bf16[64,256]{1,0:T(8,128)(2,1)} %copy-done.32) | copy-start | bytes 98308
  89.7 46.5 %collective-permute-start = (bf16[1,1,128,256]{3,2,1,0:T(8,128)(2,1)}, bf16[1,1,128,256]{3,2,1,0:T(8,128)(2,1)}, u32[]{:S(2)}, u32[]{:S(2)}) collective-permute-start(bf16[1,1,128,256]{3,2,1,0:T(8,128)(2,1)} %get-tuple-element.12), channel_id=1, source_target_pairs={{0,1},{1,2},{2,3},{3,4},{4,5},{5,6},{6,7},{8,9},{9,10},{10,11},{11... | collective-permute-start | bytes 196616 | tf_op jit(solution)/shard_map/ppermute | solution.py:15
  131.5 6.5 %copy-start.2 = (bf16[1,8,128,256]{3,2,1,0:T(8,128)(2,1)S(1)}, bf16[1,8,128,256]{3,2,1,0:T(8,128)(2,1)}, u32[]{:S(2)}) copy-start(bf16[1,8,128,256]{3,2,1,0:T(8,128)(2,1)} %copy-done.1) | copy-start | bytes 1572868
  131.5 6.5 %collective-permute-start.1 = (bf16[1,1,128,256]{3,2,1,0:T(8,128)(2,1)}, bf16[1,1,128,256]{3,2,1,0:T(8,128)(2,1)S(1)}, u32[]{:S(2)}, u32[]{:S(2)}) collective-permute-start(bf16[1,1,128,256]{3,2,1,0:T(8,128)(2,1)} %get-tuple-element.13), channel_id=1, source_target_pairs={{1,0},{2,1},{3,2},{4,3},{5,4},{6,5},{7,6},{9,8},{10,9},{11,10},{12... | collective-permute-start | bytes 196616 | tf_op jit(solution)/shard_map/ppermute | solution.py:17
  144.1 2.6 %copy-start.15 = (bf16[3,3,256,256]{3,2,1,0:T(8,128)(2,1)S(1)}, bf16[3,3,256,256]{3,2,1,0:T(8,128)(2,1)}, u32[]{:S(2)}) copy-start(bf16[3,3,256,256]{3,2,1,0:T(8,128)(2,1)} %all-gather.10.cloned.1.call-done) | copy-start | bytes 3538948
  149.4 4.3 %copy-start.31 = (bf16[512,256]{1,0:T(8,128)(2,1)}, bf16[512,256]{1,0:T(8,128)(2,1)S(1)}, u32[]{:S(2)}) copy-start(bf16[512,256]{1,0:T(8,128)(2,1)S(1)} %fusion.5) | copy-start | bytes 786436
  160.2 22.8 %copy-start.30 = (bf16[1,4,64,256]{3,2,1,0:T(8,128)(2,1)S(1)}, bf16[1,4,64,256]{3,2,1,0:T(8,128)(2,1)}, u32[]{:S(2)}) copy-start(bf16[1,4,64,256]{3,2,1,0:T(8,128)(2,1)} %get-tuple-element.26) | copy-start | bytes 393220
  160.2 24.0 %copy-start.29 = (bf16[1,4,64,256]{3,2,1,0:T(8,128)(2,1)S(1)}, bf16[1,4,64,256]{3,2,1,0:T(8,128)(2,1)}, u32[]{:S(2)}) copy-start(bf16[1,4,64,256]{3,2,1,0:T(8,128)(2,1)} %get-tuple-element.27) | copy-start | bytes 393220
  161.3 25.3 %copy-start.28 = (bf16[1,4,64,256]{3,2,1,0:T(8,128)(2,1)S(1)}, bf16[1,4,64,256]{3,2,1,0:T(8,128)(2,1)}, u32[]{:S(2)}) copy-start(bf16[1,4,64,256]{3,2,1,0:T(8,128)(2,1)} %get-tuple-element.25) | copy-start | bytes 393220
  183.0 3.6 %copy-start.14 = (bf16[3,3,256,256]{3,2,1,0:T(8,128)(2,1)S(1)}, bf16[3,3,256,256]{3,2,1,0:T(8,128)(2,1)}, u32[]{:S(2)}) copy-start(bf16[3,3,256,256]{3,2,1,0:T(8,128)(2,1)} %all-gather.8.cloned.1.call-done) | copy-start | bytes 3538948
  184.2 2.6 %copy-start.27 = (bf16[1,4,64,256]{3,2,1,0:T(8,128)(2,1)S(1)}, bf16[1,4,64,256]{3,2,1,0:T(8,128)(2,1)}, u32[]{:S(2)}) copy-start(bf16[1,4,64,256]{3,2,1,0:T(8,128)(2,1)} %get-tuple-element.24) | copy-start | bytes 393220
  (26 other events, 30.4 us)
Sparse Core Ops, SparseCore 0:
  10.1 44.0 all-gather.5
  56.4 42.2 all-gather.11
  100.9 40.0 all-gather.9
  143.0 39.8 all-gather.7
